TPU v7x, 32 devices: a whole 2x2x4 slice. The times are simulated.
32 devices in a mesh: section: 4 (over y, core), dp: 2 (over x), tensor: 4 (over z).
Axes of the slice: x: 2, y: 2, z: 4, core: 2. Of those that a mesh axis runs over, the one named last changes fastest.
Arguments:
- shadow_weight_copy: bfloat16 [4, 4096, 4096], P('section', None, 'tensor'), may hold values from -6 to 6
- newest_weight_version: bfloat16 [4, 4096, 4096], P('section', 'dp', 'tensor'), may hold values from -6 to 6
- momentum: bfloat16 [4, 4096, 4096], P('section', 'dp', 'tensor'), may hold values from -3 to 3
- pending_section_input: bfloat16 [2, 4, 64, 4096], P('dp', 'section', None, 'tensor'), may hold values from -16 to 16
- incoming_micro_input: bfloat16 [2, 3, 64, 4096], P('dp', None, None, 'tensor'), may hold values from -16 to 16
- pending_output_gradient: bfloat16 [2, 4, 64, 4096], P('dp', 'section', None, 'tensor'), may hold values from -16 to 16
- loss_gradient_rows: bfloat16 [2, 3, 64, 4096], P('dp', None, None, 'tensor'), may hold values from -16 to 16
- stashed: bfloat16 [2, 4, 4, 64, 4096], P('dp', 'section', None, None, 'tensor'), may hold values from -16 to 16
Outputs:
- forward_out: bfloat16 [2, 4, 4, 64, 4096], P('dp', 'section', None, None, 'tensor')
- backward_out: bfloat16 [2, 4, 4, 64, 4096], P('dp', 'section', None, None, 'tensor')
- w_next: bfloat16 [4, 4096, 4096], P('section', 'dp', 'tensor')
- m_next: bfloat16 [4, 4096, 4096], P('section', 'dp', 'tensor')
All inputs are finite; a program needn't handle non-finite values.
Results may differ from a plain program's by a relative error of at most 0.025.
Values may be sent and summed in bfloat16 or wider, within the bound.
No kernel may reach another device: no remote copies, remote signals or barrier semaphores. Data moves between devices by JAX's collectives and lax.ppermute only.
A program may use at most 128 MiB of HBM per device.

v0:
```python
import math

import jax
import jax.numpy as jnp
from jax import lax
from jax.sharding import PartitionSpec as P

EPSILON = 1e-06
MOMENTUM_RATE = 0.9
LEARNING_RATE = 0.05


def shifted(block, axis, distance):
    devices = range(lax.axis_size(axis))
    route = [(i - distance, i) for i in devices if i - distance in devices]
    return lax.ppermute(block, axis, route)


def normalized(values):
    factor = lax.rsqrt(jnp.mean(values * values, axis=-1, keepdims=True) + EPSILON)
    return (values * factor, factor)


def body(
    shadow_weight_copy,
    newest_weight_version,
    momentum,
    pending_section_input,
    incoming_micro_input,
    pending_output_gradient,
    loss_gradient_rows,
    stashed,
):
    weight = shadow_weight_copy[0]
    extent = weight.shape[0]
    own_cols = weight.shape[1]
    root_width = math.sqrt(extent)
    tick_count = stashed.shape[2]
    section_count = lax.axis_size("section")
    is_first = lax.axis_index("section") == 0
    is_last = lax.axis_index("section") == section_count - 1
    col_start = lax.axis_index("tensor") * own_cols
    current_input = pending_section_input[0, 0]
    current_gradient = pending_output_gradient[0, 0]
    forward_list = []
    backward_list = []
    kept_list = []
    grad_list = []
    for tick_index in range(tick_count):
        if tick_index > 0:
            from_below = shifted(forward_list[-1], "section", 1)
            current_input = jnp.where(is_first, incoming_micro_input[0, tick_index - 1], from_below)
            from_above = shifted(backward_list[-1], "section", -1)
            current_gradient = jnp.where(is_last, loss_gradient_rows[0, tick_index - 1], from_above)
        whole_x, whole_kept = (
            lax.all_gather(current_input, "tensor", axis=1, tiled=True),
            lax.all_gather(stashed[0, 0, tick_index], "tensor", axis=1, tiled=True),
        )
        x_hat, unused = normalized(whole_x.astype(jnp.float32))
        branch = (
            jnp.dot(x_hat.astype(jnp.bfloat16), weight, preferred_element_type=jnp.float32)
            / root_width
        )
        forward_list.append((current_input.astype(jnp.float32) + branch).astype(jnp.bfloat16))
        kept_hat, kept_factor = normalized(whole_kept.astype(jnp.float32))
        partial_value = (
            lax.dot_general(
                current_gradient,
                weight,
                (((1,), (1,)), ((), ())),
                preferred_element_type=jnp.float32,
            )
            / root_width
        ).astype(jnp.bfloat16)
        own_hat = lax.dynamic_slice_in_dim(kept_hat, col_start, own_cols, 1)
        own_grad = lax.psum_scatter(
            partial_value, "tensor", scatter_dimension=1, tiled=True
        ).astype(jnp.float32)
        inner_dot = lax.psum(jnp.sum(own_grad * own_hat, axis=-1, keepdims=True), "tensor") / extent
        input_grad = (
            current_gradient.astype(jnp.float32) + (own_grad - own_hat * inner_dot) * kept_factor
        )
        backward_list.append(input_grad.astype(jnp.bfloat16))
        kept_list.append(kept_hat.astype(jnp.bfloat16))
        grad_list.append(current_gradient)
    kept_rows = jnp.concatenate(kept_list, axis=0)
    grad_rows = jnp.concatenate(grad_list, axis=0)
    replica_term = (
        lax.dot_general(
            kept_rows, grad_rows, (((0,), (0,)), ((), ())), preferred_element_type=jnp.float32
        )
        / root_width
    ).astype(jnp.bfloat16)
    summed = lax.psum_scatter(replica_term, "dp", scatter_dimension=0, tiled=True).astype(
        jnp.float32
    )
    velocity = MOMENTUM_RATE * momentum[0].astype(jnp.float32) + summed
    w_next = (newest_weight_version[0].astype(jnp.float32) - LEARNING_RATE * velocity).astype(
        jnp.bfloat16
    )[None]
    m_next = velocity.astype(jnp.bfloat16)[None]
    forward_out = jnp.stack(forward_list, axis=0)[None, None]
    backward_out = jnp.stack(backward_list, axis=0)[None, None]
    return (forward_out, backward_out, w_next, m_next)


def solution(mesh):
    return jax.shard_map(
        body,
        mesh=mesh,
        in_specs=(
            P("section", None, "tensor"),
            P("section", "dp", "tensor"),
            P("section", "dp", "tensor"),
            P("dp", "section", None, "tensor"),
            P("dp", None, None, "tensor"),
            P("dp", "section", None, "tensor"),
            P("dp", None, None, "tensor"),
            P("dp", "section", None, None, "tensor"),
        ),
        out_specs=(
            P("dp", "section", None, None, "tensor"),
            P("dp", "section", None, None, "tensor"),
            P("section", "dp", "tensor"),
            P("section", "dp", "tensor"),
        ),
        check_vma=False,
    )
```

profile of v0, /device:TPU:0, one launch (start us, length us, event | category | flops | bytes accessed | tf_op | source)
XLA Modules:
  0.0 335.9 jit_solution(7891010142634172775)
XLA Ops:
  7.2 7.0 %fusion.39 = bf16[64,4096]{1,0:T(8,128)(2,1)} fusion(bf16[1,4096,1024]{2,1,0:T(8,128)(2,1)} %param.8, bf16[1,1,64,1024]{3,2,1,0:T(8,128)(2,1)} %param.13), kind=kOutput, calls=%fused_computation.28 | convolution fusion | flops 537395200 | bytes 9043968 | tf_op jit(solution)/shard_map/dot_general | solution.py:67
  14.3 22.5 %all-gather.3 = bf16[1,1,1,64,4096]{4,3,2,1,0:T(8,128)(2,1)S(1)} all-gather(bf16[1,1,1,64,1024]{4,3,2,1,0:T(8,128)(2,1)S(1)} %get-tuple-element.14), channel_id=5, replica_groups=mesh['section'=4,'dp'=2,'tensor'=4] {'tensor'}, dimensions={4}, use_global_device_ids=true | all-gather | bytes 655360 | tf_op jit(solution)/shard_map/all_gather | solution.py:57
  37.1 15.9 %all-gather.1 = bf16[1,1,1,64,4096]{4,3,2,1,0:T(8,128)(2,1)S(1)} all-gather(bf16[1,1,1,64,1024]{4,3,2,1,0:T(8,128)(2,1)S(1)} %get-tuple-element.16), channel_id=3, replica_groups=mesh['section'=4,'dp'=2,'tensor'=4] {'tensor'}, dimensions={4}, use_global_device_ids=true | all-gather | bytes 655360 | tf_op jit(solution)/shard_map/all_gather | solution.py:57
  53.2 15.7 %all-gather.2 = bf16[1,1,1,64,4096]{4,3,2,1,0:T(8,128)(2,1)S(1)} all-gather(bf16[1,1,1,64,1024]{4,3,2,1,0:T(8,128)(2,1)S(1)} %get-tuple-element.15), channel_id=4, replica_groups=mesh['section'=4,'dp'=2,'tensor'=4] {'tensor'}, dimensions={4}, use_global_device_ids=true | all-gather | bytes 655360 | tf_op jit(solution)/shard_map/all_gather | solution.py:57
  69.2 1.0 fusion.97
  70.2 9.0 %psum.28 = f32[64,1]{0,1:T(1,128)S(1)} all-reduce(f32[64,1]{0,1:T(1,128)S(1)} %bitcast.156), channel_id=1, replica_groups=mesh['section'=4,'dp'=2,'tensor'=4] {'tensor'}, use_global_device_ids=true, to_apply=%region_7.8 | all-reduce | flops 64 | bytes 512 | tf_op jit(solution)/shard_map/psum | solution.py:79
  79.2 1.0 fusion.100
  80.2 1.3 collective-permute-start.3
  81.7 1.7 collective-permute-done.3
  83.5 0.9 bitcast_select_fusion.2
  84.4 6.8 %fusion.36 = bf16[64,4096]{1,0:T(8,128)(2,1)} fusion(bf16[64,1024]{1,0:T(8,128)(2,1)S(1)} %bitcast_select_fusion.2, bf16[1,4096,1024]{2,1,0:T(8,128)(2,1)} %param.8), kind=kOutput, calls=%fused_computation.27 | convolution fusion | flops 537395200 | bytes 9043968 | tf_op jit(solution)/shard_map/dot_general | solution.py:67
  91.3 1.0 fusion.130
  92.3 21.8 %reduce-scatter.8.cloned.1.call-done = bf16[64,1024]{1,0:T(8,128)(2,1)} async-done(((bf16[64,4096]{1,0:T(8,128)(2,1)}), bf16[64,1024]{1,0:T(8,128)(2,1)}) %reduce-scatter.8.cloned.1.call-update) | async-done | bytes 131088 | tf_op jit(solution)/shard_map/reduce_scatter | solution.py:76
  114.2 1.0 fusion.101
  115.2 8.6 %psum.29 = f32[64,1]{0,1:T(1,128)S(1)} all-reduce(f32[64,1]{0,1:T(1,128)S(1)} %bitcast.157), channel_id=1, replica_groups=mesh['section'=4,'dp'=2,'tensor'=4] {'tensor'}, use_global_device_ids=true, to_apply=%region_11.12 | all-reduce | flops 64 | bytes 512 | tf_op jit(solution)/shard_map/psum | solution.py:79
  123.8 1.0 fusion.104
  124.9 1.3 collective-permute-start.4
  126.2 15.9 %all-gather.4 = bf16[1,1,1,64,4096]{4,3,2,1,0:T(8,128)(2,1)S(1)} all-gather(bf16[1,1,1,64,1024]{4,3,2,1,0:T(8,128)(2,1)S(1)} %get-tuple-element.17), channel_id=6, replica_groups=mesh['section'=4,'dp'=2,'tensor'=4] {'tensor'}, dimensions={4}, use_global_device_ids=true | all-gather | bytes 655360 | tf_op jit(solution)/shard_map/all_gather | solution.py:57
  142.0 0.9 bitcast_select_fusion.1
  143.0 6.8 %fusion.33 = bf16[64,4096]{1,0:T(8,128)(2,1)} fusion(bf16[64,1024]{1,0:T(8,128)(2,1)S(1)} %bitcast_select_fusion.1, bf16[1,4096,1024]{2,1,0:T(8,128)(2,1)} %param.8), kind=kOutput, calls=%fused_computation.26 | convolution fusion | flops 537395200 | bytes 9043968 | tf_op jit(solution)/shard_map/dot_general | solution.py:67
  150.1 1.0 fusion.131
  151.1 21.0 %reduce-scatter.10.cloned.1.call-done = bf16[64,1024]{1,0:T(8,128)(2,1)} async-done(((bf16[64,4096]{1,0:T(8,128)(2,1)}), bf16[64,1024]{1,0:T(8,128)(2,1)}) %reduce-scatter.10.cloned.1.call-update) | async-done | bytes 131088 | tf_op jit(solution)/shard_map/reduce_scatter | solution.py:76
  172.1 1.0 fusion.105
  173.1 8.6 %psum.30 = f32[64,1]{0,1:T(1,128)S(1)} all-reduce(f32[64,1]{0,1:T(1,128)S(1)} %bitcast.158), channel_id=1, replica_groups=mesh['section'=4,'dp'=2,'tensor'=4] {'tensor'}, use_global_device_ids=true, to_apply=%region_15.16 | all-reduce | flops 64 | bytes 512 | tf_op jit(solution)/shard_map/psum | solution.py:79
  181.8 1.0 fusion.108
  182.8 1.3 collective-permute-start.5
  184.1 1.9 collective-permute-done.5
  187.0 6.8 %fusion.30 = bf16[64,4096]{1,0:T(8,128)(2,1)} fusion(bf16[64,1024]{1,0:T(8,128)(2,1)S(1)} %bitcast_select_fusion, bf16[1,4096,1024]{2,1,0:T(8,128)(2,1)} %param.8), kind=kOutput, calls=%fused_computation.25 | convolution fusion | flops 537395200 | bytes 9043968 | tf_op jit(solution)/shard_map/dot_general | solution.py:67
  194.3 6.8 %multiply_convert_fusion = bf16[4096,1024]{1,0:T(8,128)(2,1)} fusion(bf16[64,4096]{1,0:T(8,128)(2,1)S(1)} %get-tuple-element.12, bf16[64,4096]{1,0:T(8,128)(2,1)} %get-tuple-element.10, bf16[64,4096]{1,0:T(8,128)(2,1)} %get-tuple-element.8, bf16[64,4096]{1,0:T(8,128)(2,1)S(1)} %get-tuple-element.6, bf16[64,1024]{1,0:T(8,128)(2,1)S(1)} %bitcast_select_fusion, ...), kind=kOutput, calls=%fused_computation | convolution fusion | flops 2166358016 | bytes 11010048 | tf_op jit(solution)/shard_map/dot_general | solution.py:89
  202.0 19.3 %all-gather = bf16[1,1,64,4096]{3,2,1,0:T(8,128)(2,1)S(1)} all-gather(bf16[1,1,64,1024]{3,2,1,0:T(8,128)(2,1)S(1)} %copy-done), channel_id=2, replica_groups=mesh['section'=4,'dp'=2,'tensor'=4] {'tensor'}, dimensions={3}, use_global_device_ids=true | all-gather | bytes 655360 | tf_op jit(solution)/shard_map/all_gather | solution.py:56
  221.5 5.1 %fusion.66 = bf16[64,1024]{1,0:T(8,128)(2,1)S(1)} fusion(bf16[1,4096,1024]{2,1,0:T(8,128)(2,1)} %param.8, bf16[1,1,64,4096]{3,2,1,0:T(8,128)(2,1)S(1)} %all-gather, f32[64]{0:T(128)S(1)} %add_rsqrt_fusion.7, bf16[1,1,64,1024]{3,2,1,0:T(8,128)(2,1)S(1)} %copy-done), kind=kOutput, calls=%fused_computation.59 | convolution fusion | flops 537919488 | bytes 9175296 | tf_op jit(solution)/shard_map/dot_general | solution.py:61
  226.6 3.1 collective-permute-start
  229.7 1.0 collective-permute-done
  230.7 15.9 %all_gather.25 = bf16[64,4096]{1,0:T(8,128)(2,1)S(1)} all-gather(bf16[64,1024]{1,0:T(8,128)(2,1)S(1)} %bitcast_select_fusion.5), channel_id=1, replica_groups=mesh['section'=4,'dp'=2,'tensor'=4] {'tensor'}, dimensions={1}, use_global_device_ids=true | all-gather | bytes 655360 | tf_op jit(solution)/shard_map/all_gather | solution.py:56
  246.8 5.4 %add_convert_fusion.2 = bf16[64,1024]{1,0:T(8,128)(2,1)S(1)} fusion(bf16[64,1024]{1,0:T(8,128)(2,1)S(1)} %bitcast_select_fusion.5, bf16[1,4096,1024]{2,1,0:T(8,128)(2,1)} %param.8, bf16[64,4096]{1,0:T(8,128)(2,1)S(1)} %all_gather.25, f32[64]{0:T(128)S(1)} %add_rsqrt_fusion.6), kind=kOutput, calls=%fused_computation.112 | convolution fusion | flops 537919488 | bytes 9175296 | tf_op jit(solution)/shard_map/dot_general | solution.py:61
  252.3 2.1 collective-permute-start.1
  254.4 1.0 collective-permute-done.1
  255.4 15.9 %all_gather.26 = bf16[64,4096]{1,0:T(8,128)(2,1)S(1)} all-gather(bf16[64,1024]{1,0:T(8,128)(2,1)S(1)} %bitcast_select_fusion.4), channel_id=1, replica_groups=mesh['section'=4,'dp'=2,'tensor'=4] {'tensor'}, dimensions={1}, use_global_device_ids=true | all-gather | bytes 655360 | tf_op jit(solution)/shard_map/all_gather | solution.py:56
  271.5 1.6 add_convert_fusion.1
  273.1 4.9 %collective-permute-start.2 = (bf16[64,1024]{1,0:T(8,128)(2,1)S(1)}, bf16[64,1024]{1,0:T(8,128)(2,1)S(1)}, u32[]{:S(2)}, u32[]{:S(2)}) collective-permute-start(bf16[64,1024]{1,0:T(8,128)(2,1)S(1)} %add_convert_fusion.1), channel_id=1, source_target_pairs={{0,8},{8,16},{16,24},{1,9},{9,17},{17,25},{2,10},{10,18},{18,26},{... | collective-permute-start | bytes 393224 | tf_op jit(solution)/shard_map/ppermute | solution.py:16
  278.0 1.0 collective-permute-done.2
  279.0 16.2 %all_gather.27 = bf16[64,4096]{1,0:T(8,128)(2,1)S(1)} all-gather(bf16[64,1024]{1,0:T(8,128)(2,1)S(1)} %bitcast_select_fusion.3), channel_id=1, replica_groups=mesh['section'=4,'dp'=2,'tensor'=4] {'tensor'}, dimensions={1}, use_global_device_ids=true | all-gather | bytes 655360 | tf_op jit(solution)/shard_map/all_gather | solution.py:56
  295.5 1.7 fusion.113
  298.0 1.0 fusion.109
  299.0 10.3 %psum.31 = f32[64,1]{0,1:T(1,128)S(1)} all-reduce(f32[64,1]{0,1:T(1,128)S(1)} %bitcast.159), channel_id=1, replica_groups=mesh['section'=4,'dp'=2,'tensor'=4] {'tensor'}, use_global_device_ids=true, to_apply=%region_19.20 | all-reduce | flops 64 | bytes 512 | tf_op jit(solution)/shard_map/psum | solution.py:79
  309.3 1.0 fusion.114
  311.2 9.8 %reduce-scatter.14.cloned.1.call-done = bf16[2048,1024]{1,0:T(8,128)(2,1)} async-done(((bf16[4096,1024]{1,0:T(8,128)(2,1)}), bf16[2048,1024]{1,0:T(8,128)(2,1)}) %reduce-scatter.14.cloned.1.call-update) | async-done | bytes 4194320 | tf_op jit(solution)/shard_map/reduce_scatter | solution.py:94
  321.1 8.3 %fusion.42 = (bf16[1,2048,1024]{2,1,0:T(8,128)(2,1)}, bf16[1,2048,1024]{2,1,0:T(8,128)(2,1)}) fusion(bf16[2048,1024]{1,0:T(8,128)(2,1)} %reduce-scatter.14.cloned.1.call-done, bf16[1,2048,1024]{2,1,0:T(8,128)(2,1)} %param.10, bf16[1,2048,1024]{2,1,0:T(8,128)(2,1)} %param.9), kind=kLoop, calls=%fused_computation.29 | loop fusion | flops 18874368 | bytes 20971520 | tf_op jit(solution)/shard_map/broadcast_in_dim | solution.py:101
  (55 shorter events, 6.3 us)
Async XLA Ops:
  7.2 72.0 %copy-start.1 = (bf16[1,1,64,1024]{3,2,1,0:T(8,128)(2,1)S(1)}, bf16[1,1,64,1024]{3,2,1,0:T(8,128)(2,1)}, u32[]{:S(2)}) copy-start(bf16[1,1,64,1024]{3,2,1,0:T(8,128)(2,1)} %param.13) | copy-start | bytes 393220
  7.2 7.1 %copy-start.2 = (bf16[1,1,4,64,1024]{4,3,2,1,0:T(8,128)(2,1)S(1)}, bf16[1,1,4,64,1024]{4,3,2,1,0:T(8,128)(2,1)}, u32[]{:S(2)}) copy-start(bf16[1,1,4,64,1024]{4,3,2,1,0:T(8,128)(2,1)} %param.15) | copy-start | bytes 1572868
  7.2 62.0 %reduce-scatter.6.cloned.1.call-start = ((), (), s32[]{:S(2)}) async-start(), calls=%async_computation.5 | async-start | bytes 655360 | tf_op jit(solution)/shard_map/reduce_scatter | solution.py:76
  14.2 99.9 %reduce-scatter.8.cloned.1.call-start = ((), (), s32[]{:S(2)}) async-start(), calls=%async_computation.6 | async-start | bytes 655360 | tf_op jit(solution)/shard_map/reduce_scatter | solution.py:76
  80.2 3.2 collective-permute-start.3
  91.3 80.8 %reduce-scatter.10.cloned.1.call-start = ((), (), s32[]{:S(2)}) async-start(), calls=%async_computation.7 | async-start | bytes 655360 | tf_op jit(solution)/shard_map/reduce_scatter | solution.py:76
  124.9 17.2 %collective-permute-start.4 = (bf16[64,1024]{1,0:T(8,128)(2,1)S(1)}, bf16[64,1024]{1,0:T(8,128)(2,1)S(1)}, u32[]{:S(2)}, u32[]{:S(2)}) collective-permute-start(bf16[64,1024]{1,0:T(8,128)(2,1)S(1)} %fusion.104), channel_id=1, source_target_pairs={{8,0},{16,8},{24,16},{9,1},{17,9},{25,17},{10,2},{18,10},{26,18},{... | collective-permute-start | bytes 393224 | tf_op jit(solution)/shard_map/ppermute | solution.py:16
  149.8 148.2 %reduce-scatter.12.cloned.1.call-start = ((), (), s32[]{:S(2)}) async-start(), calls=%async_computation.8 | async-start | bytes 655360 | tf_op jit(solution)/shard_map/reduce_scatter | solution.py:76
  182.8 3.2 collective-permute-start.5
  193.8 127.2 %reduce-scatter.14.cloned.1.call-start = ((), (), s32[]{:S(2)}) async-start(), calls=%async_computation.9 | async-start | bytes 12582912 | tf_op jit(solution)/shard_map/reduce_scatter | solution.py:94
  201.1 0.9 copy-start
  221.5 9.2 %copy-start.3 = (bf16[1,3,64,1024]{3,2,1,0:T(8,128)(2,1)S(1)}, bf16[1,3,64,1024]{3,2,1,0:T(8,128)(2,1)}, u32[]{:S(2)}) copy-start(bf16[1,3,64,1024]{3,2,1,0:T(8,128)(2,1)} %param.12) | copy-start | bytes 1179652
  226.6 4.1 %collective-permute-start = (bf16[64,1024]{1,0:T(8,128)(2,1)S(1)}, bf16[64,1024]{1,0:T(8,128)(2,1)S(1)}, u32[]{:S(2)}, u32[]{:S(2)}) collective-permute-start(bf16[64,1024]{1,0:T(8,128)(2,1)S(1)} %fusion.66), channel_id=1, source_target_pairs={{0,8},{8,16},{16,24},{1,9},{9,17},{17,25},{2,10},{10,18},{18,26},{... | collective-permute-start | bytes 393224 | tf_op jit(solution)/shard_map/ppermute | solution.py:16
  230.7 40.8 %slice-start = ((s8[8388608]{0:T(1024)(128)(4,1)}), s8[4194304]{0:T(1024)(128)(4,1)S(1)}, s32[]{:S(2)}) async-start(s8[8388608]{0:T(1024)(128)(4,1)} %bitcast.147), calls=%async_computation.10 | async-start | bytes 8388608
  246.8 24.6 %slice-start.1 = ((s8[8388608]{0:T(1024)(128)(4,1)}), s8[4194304]{0:T(1024)(128)(4,1)S(1)}, s32[]{:S(2)}) async-start(s8[8388608]{0:T(1024)(128)(4,1)} %bitcast.147), calls=%async_computation.11 | async-start | bytes 8388608
  252.3 3.1 collective-permute-start.1
  273.1 5.9 %collective-permute-start.2 = (bf16[64,1024]{1,0:T(8,128)(2,1)S(1)}, bf16[64,1024]{1,0:T(8,128)(2,1)S(1)}, u32[]{:S(2)}, u32[]{:S(2)}) collective-permute-start(bf16[64,1024]{1,0:T(8,128)(2,1)S(1)} %add_convert_fusion.1), channel_id=1, source_target_pairs={{0,8},{8,16},{16,24},{1,9},{9,17},{17,25},{2,10},{10,18},{18,26},{... | collective-permute-start | bytes 393224 | tf_op jit(solution)/shard_map/ppermute | solution.py:16
Sparse Core Ops, SparseCore 0:
  14.4 27.4 reduce-scatter.5
  91.4 22.7 reduce-scatter.7
  149.9 22.1 reduce-scatter.9
  194.0 25.5 reduce-scatter.11
  221.7 99.3 reduce-scatter.13
where the time goes:
time: 337 us; the launch traced here: 336 us
  blocking collectives  174 us (52%)
  waiting for transfers between devices  59.4 us (18%)
  matrix products  48.1 us (14%)
  other arithmetic  25.3 us (8%)
  starting transfers between devices  14.4 us (4%)
  between operations  14 us (4%)
    all_gather x4, blocking collectives, body(): lax.all_gather(stashed[0, 0, tick_index], 'tensor', axis=1, tiled=True)  70.1 us
    all_gather x4, blocking collectives, body(): lax.all_gather(current_input, 'tensor', axis=1, tiled=True)  67.3 us
    reduce_scatter x4, waiting for transfers between devices, body(): lax.psum_scatter(partial_value, 'tensor', scatter_dimension=1, tiled=True)  42.9 us
    psum x4, blocking collectives, body(): lax.psum(jnp.sum(own_grad * own_hat, axis=-1, keepdims=True), 'tensor')  36.5 us
    dot_general x4, matrix products, body(): lax.dot_general(current_gradient, weight, (((1,), (1,)), ((), ())), prefe...  27.5 us
    ppermute x6, starting transfers between devices, shifted(): return lax.ppermute(block, axis, route)  14 us
    dot_general x4, matrix products, body(): jnp.dot(x_hat.astype(jnp.bfloat16), weight, preferred_element_type=jnp.fl...  13.8 us
    reduce_scatter x1, waiting for transfers between devices, body(): lax.psum_scatter(replica_term, 'dp', scatter_dimension=0, tiled=True)  9.84 us
  transfers between devices with their start and end apart: 11, of which 8 were waited for; matrix products, arithmetic and copies ran while one was open for 9% of the time, Pallas kernels for 0%

commit v1 on v0

v1 whole, which is shorter than its diff:
```python
import functools
import math

import jax
import jax.numpy as jnp
from jax import lax
from jax.experimental import pallas as pl
from jax.experimental.pallas import tpu as pltpu
from jax.sharding import PartitionSpec as P

EPSILON = 1e-06
MOMENTUM_RATE = 0.9
LEARNING_RATE = 0.05
LANES = 128
MIB = 1 << 20

BF16 = jnp.bfloat16
F32 = jnp.float32


def cyclic(block, distance):
    count = lax.axis_size("tensor")
    return lax.ppermute(block, "tensor", [(i, (i + distance) % count) for i in range(count)])


def gathered(block):
    return [block] + [cyclic(block, d) for d in range(1, lax.axis_size("tensor"))]


def gathered_from_below(block):
    sections, count = lax.axis_size("section"), lax.axis_size("tensor")
    result = []
    for d in range(count):
        route = [
            (s * count + t, ((s + 1) % sections) * count + (t + d) % count)
            for s in range(sections)
            for t in range(count)
        ]
        result.append(lax.ppermute(block, ("section", "tensor"), route))
    return result


def from_above(block):
    sections = lax.axis_size("section")
    return lax.ppermute(block, "section", [(s, (s - 1) % sections) for s in range(sections)])


def dp_cyclic(block, distance):
    count = lax.axis_size("dp")
    return lax.ppermute(block, "dp", [(i, (i + distance) % count) for i in range(count)])


def rows_of(w_ref, index, size):
    return w_ref[pl.ds(pl.multiple_of(index * size, size), size), :]


def row_factor(blocks, extent):
    total = sum(jnp.sum(b * b, axis=-1, keepdims=True) for b in blocks)
    return lax.rsqrt(total / extent + EPSILON)


def forward_kernel(count, with_payload, where_ref, w_ref, *refs):
    blocks, rest = refs[:count], refs[count:]
    extent, size = w_ref.shape[0], w_ref.shape[0] // count
    me = where_ref[0]
    acc = None
    for d in range(count):
        term = jnp.dot(
            blocks[d][...],
            rows_of(w_ref, lax.rem(me - d + count, count), size),
            preferred_element_type=F32,
        )
        acc = term if acc is None else acc + term
    factor = row_factor([b[...].astype(F32) for b in blocks], extent)
    out = (blocks[0][...].astype(F32) + acc * (factor * (1.0 / math.sqrt(extent)))).astype(BF16)
    if with_payload:
        incoming_ref, out_ref, payload_ref = rest
        payload_ref[...] = jnp.where(where_ref[2] == 1, incoming_ref[...], out)
    else:
        (out_ref,) = rest
    out_ref[...] = out


def backward_kernel(count, replicas, where_ref, w_ref, grad_ref, *refs):
    kept = refs[:count]
    payloads = refs[count : 2 * count]
    factor_ref = refs[2 * count]
    hats = refs[2 * count + 1 :]
    extent, size = w_ref.shape[0], w_ref.shape[0] // count
    root = 1.0 / math.sqrt(extent)
    me, rank = where_ref[0], where_ref[3]
    wide = [b[...].astype(F32) for b in kept]
    factor = row_factor(wide, extent)
    factor_ref[...] = jnp.broadcast_to(factor, factor_ref.shape)
    grad = grad_ref[...]
    total = None
    for d in range(count):
        term = (
            lax.dot_general(
                grad,
                rows_of(w_ref, lax.rem(me + d, count), size),
                (((1,), (1,)), ((), ())),
                preferred_element_type=F32,
            )
            * root
        ).astype(BF16)
        payloads[d][:, :size] = term
        part = jnp.sum(term.astype(F32) * wide[(count - d) % count], axis=-1, keepdims=True)
        total = part if total is None else total + part
    total = total * factor
    high = total.astype(BF16)
    middle = (total - high.astype(F32)).astype(BF16)
    low = (total - high.astype(F32) - middle.astype(F32)).astype(BF16)
    lane = lax.broadcasted_iota(jnp.int32, (grad.shape[0], LANES), 1)
    tail = jnp.where(
        lane == 0,
        high.astype(F32),
        jnp.where(lane == 1, middle.astype(F32), jnp.where(lane == 2, low.astype(F32), 0.0)),
    ).astype(BF16)
    for d in range(count):
        payloads[d][:, size:] = tail
    hat = [(w * factor).astype(BF16) for w in wide]
    per = count // replicas
    for r in range(replicas):
        owner = lax.rem(rank + r, replicas)
        for k in range(per):
            distance = lax.rem(me - (owner * per + k) + count, count)
            chosen = hat[0]
            for d in range(1, count):
                chosen = jnp.where(distance == d, hat[d], chosen)
            hats[r][k] = chosen


def combine_kernel(count, with_payload, where_ref, grad_ref, kept_ref, factor_ref, *refs):
    parts, rest = refs[:count], refs[count:]
    size = grad_ref.shape[1]
    own = sum(p[:, :size].astype(F32) for p in parts)
    inner = sum(jnp.sum(p[:, size:].astype(F32), axis=-1, keepdims=True) for p in parts)
    inner = inner / (size * count)
    factor = factor_ref[:, :1]
    hat = kept_ref[...].astype(F32) * factor
    out = (grad_ref[...].astype(F32) + (own - hat * inner) * factor).astype(BF16)
    if with_payload:
        loss_ref, out_ref, payload_ref = rest
        payload_ref[...] = jnp.where(where_ref[1] == 1, loss_ref[...], out)
    else:
        (out_ref,) = rest
    out_ref[...] = out


def update_kernel(pieces, root, *refs):
    hats, grads = refs[:pieces], refs[pieces : 2 * pieces]
    w_ref, m_ref, w_out, m_out, hat_all, grad_all = refs[2 * pieces :]
    rows = grads[0].shape[0]

    @pl.when(pl.program_id(0) == 0)
    def _():
        for i in range(pieces):
            size = hats[i].shape[2]
            for k in range(hats[i].shape[0]):
                hat_all[i * rows : (i + 1) * rows, k * size : (k + 1) * size] = hats[i][k]
            grad_all[i * rows : (i + 1) * rows, :] = grads[i][...]

    tile = w_ref.shape[0]
    start = pl.multiple_of(pl.program_id(0) * tile, tile)
    summed = (
        lax.dot_general(
            hat_all[:, pl.ds(start, tile)],
            grad_all[...],
            (((0,), (0,)), ((), ())),
            preferred_element_type=F32,
        )
        * root
    )
    velocity = MOMENTUM_RATE * m_ref[...].astype(F32) + summed
    w_out[...] = (w_ref[...].astype(F32) - LEARNING_RATE * velocity).astype(BF16)
    m_out[...] = velocity.astype(BF16)


SMEM_SPEC = pl.BlockSpec(memory_space=pltpu.SMEM)
VMEM_SPEC = pl.BlockSpec(memory_space=pltpu.VMEM)


def cost(flops, moved):
    return pl.CostEstimate(flops=flops, bytes_accessed=moved, transcendentals=0)


def call(kernel, shapes, flops, limit, *operands):
    moved = sum(math.prod(o.shape) * o.dtype.itemsize for o in operands + tuple(shapes))
    return pl.pallas_call(
        kernel,
        out_shape=shapes,
        in_specs=[SMEM_SPEC] + [VMEM_SPEC] * (len(operands) - 1),
        out_specs=[VMEM_SPEC] * len(shapes),
        compiler_params=pltpu.CompilerParams(vmem_limit_bytes=limit),
        cost_estimate=cost(flops, moved),
    )(*operands)


def update(hats, grads, newest, momentum, root):
    rows, cols = newest.shape
    tile = min(256, hats[0].shape[2])
    pieces = len(hats)
    depth = pieces * grads[0].shape[0]
    whole = [pl.BlockSpec(h.shape, lambda i: (0, 0, 0)) for h in hats]
    whole += [pl.BlockSpec(g.shape, lambda i: (0, 0)) for g in grads]
    tiled = pl.BlockSpec((tile, cols), lambda i: (i, 0))
    shape = jax.ShapeDtypeStruct(newest.shape, BF16)
    return pl.pallas_call(
        functools.partial(update_kernel, pieces, root),
        grid=(rows // tile,),
        out_shape=[shape, shape],
        in_specs=whole + [tiled, tiled],
        out_specs=[tiled, tiled],
        scratch_shapes=[pltpu.VMEM((depth, rows), BF16), pltpu.VMEM((depth, cols), BF16)],
        compiler_params=pltpu.CompilerParams(vmem_limit_bytes=32 * MIB),
        cost_estimate=cost(2 * depth * rows * cols, 8 * rows * cols),
    )(*hats, *grads, newest, momentum)


def body(
    shadow_weight_copy,
    newest_weight_version,
    momentum,
    pending_section_input,
    incoming_micro_input,
    pending_output_gradient,
    loss_gradient_rows,
    stashed,
):
    weight = shadow_weight_copy[0]
    extent, size = weight.shape
    root = 1.0 / math.sqrt(extent)
    tick_count, rows = stashed.shape[2], stashed.shape[3]
    count, replicas = lax.axis_size("tensor"), lax.axis_size("dp")
    section = lax.axis_index("section")
    where = jnp.stack(
        [
            lax.axis_index("tensor"),
            (section == 0).astype(jnp.int32),
            (section == lax.axis_size("section") - 1).astype(jnp.int32),
            lax.axis_index("dp"),
        ]
    ).astype(jnp.int32)
    block = jax.ShapeDtypeStruct((rows, size), BF16)
    wide_block = jax.ShapeDtypeStruct((rows, size + LANES), BF16)
    factor_shape = jax.ShapeDtypeStruct((rows, LANES), F32)
    hat_shape = jax.ShapeDtypeStruct((count // replicas, rows, size), BF16)
    flops = 2 * rows * extent * size
    grad = pending_output_gradient[0, 0]
    x_blocks = gathered(pending_section_input[0, 0])
    forward_list, backward_list, hats, grads = [], [], [], []
    for t in range(tick_count):
        last = t == tick_count - 1
        kept = gathered(stashed[0, 0, t])
        outs = call(
            functools.partial(backward_kernel, count, replicas),
            [wide_block] * count + [factor_shape] + [hat_shape] * replicas,
            flops,
            24 * MIB,
            where,
            weight,
            grad,
            *kept,
        )
        payloads, factor, halves = outs[:count], outs[count], outs[count + 1 :]
        for r in range(replicas):
            hats.append(halves[r] if r == 0 else dp_cyclic(halves[r], r))
            grads.append(grad if r == 0 else dp_cyclic(grad, r))
        parts = [payloads[0]] + [cyclic(payloads[d], d) for d in range(1, count)]
        outs = call(
            functools.partial(forward_kernel, count, not last),
            [block] if last else [block, block],
            flops,
            24 * MIB,
            where,
            weight,
            *x_blocks,
            *([] if last else [incoming_micro_input[0, t]]),
        )
        forward_list.append(outs[0])
        if not last:
            x_blocks = gathered_from_below(outs[1])
        outs = call(
            functools.partial(combine_kernel, count, not last),
            [block] if last else [block, block],
            rows * size * 16,
            8 * MIB,
            where,
            grad,
            kept[0],
            factor,
            *parts,
            *([] if last else [loss_gradient_rows[0, t]]),
        )
        backward_list.append(outs[0])
        if not last:
            grad = from_above(outs[1])
    w_next, m_next = update(hats, grads, newest_weight_version[0], momentum[0], root)
    forward_out = jnp.stack(forward_list, axis=0)[None, None]
    backward_out = jnp.stack(backward_list, axis=0)[None, None]
    return (forward_out, backward_out, w_next[None], m_next[None])


def solution(mesh):
    return jax.shard_map(
        body,
        mesh=mesh,
        in_specs=(
            P("section", None, "tensor"),
            P("section", "dp", "tensor"),
            P("section", "dp", "tensor"),
            P("dp", "section", None, "tensor"),
            P("dp", None, None, "tensor"),
            P("dp", "section", None, "tensor"),
            P("dp", None, None, "tensor"),
            P("dp", "section", None, None, "tensor"),
        ),
        out_specs=(
            P("dp", "section", None, None, "tensor"),
            P("dp", "section", None, None, "tensor"),
            P("section", "dp", "tensor"),
            P("section", "dp", "tensor"),
        ),
        check_vma=False,
    )
```

time: 337 us -> 193 us (0.57)
  blocking collectives: 174 us -> 0 us
  starting transfers between devices: 14.4 us -> 93.9 us
  matrix products: 48.1 us -> 0 us
  Pallas kernels: 0 us -> 32.2 us
  other arithmetic: 25.3 us -> 1.8 us
  between operations: 14 us -> 0.92 us
  local copies, waits for them, and re-layouts: 0.94 us -> 5.5 us
    all_gather x8 -> x0, blocking collectives: 137 us -> none  [the longest x4 70.1 us: body(): lax.all_gather(stashed[0, 0, tick_index], 'tensor', axis=1, tiled=True)]
    ppermute x6 -> x50, starting transfers between devices: 14 us -> 93.9 us  [the longest x27 76 us: cyclic(): lax.ppermute(block, 'tensor', [(i, (i + distance) % count) for i in range...]
    reduce_scatter x5 -> x0, waiting for transfers between devices: 52.7 us -> none  [the longest x4 42.9 us: body(): lax.psum_scatter(partial_value, 'tensor', scatter_dimension=1, tiled=True)]
    ppermute x6 -> x50, waiting for transfers between devices: 6.54 us -> 58.1 us  [the longest x27 33.4 us: cyclic(): lax.ppermute(block, 'tensor', [(i, (i + distance) % count) for i in range...]
    dot_general x9 -> x0, matrix products: 48.1 us -> none  [the longest x4 27.5 us: body(): lax.dot_general(current_gradient, weight, (((1,), (1,)), ((), ())), prefe...]
    psum x4 -> x0, blocking collectives: 36.5 us -> none  [body(): lax.psum(jnp.sum(own_grad * own_hat, axis=-1, keepdims=True), 'tensor')]
    pallas_call x0 -> x13, Pallas kernels: none -> 32.2 us  [the longest x12 25.5 us: call(): pl.pallas_call(kernel, out_shape=shapes, in_specs=[SMEM_SPEC] + [VMEM_SPE...]
    broadcast_in_dim x1 -> x0, other arithmetic: 8.35 us -> none  [body(): m_next = velocity.astype(jnp.bfloat16)[None]]
  transfers between devices with their start and end apart: 11 -> 50, of which waited for: 8 -> 12; matrix products, arithmetic and copies ran while one was open for 9% -> 1% of each run, Pallas kernels for 0% -> 13%
where the time goes in v1:
time: 193 us; the launch traced here: 192 us
  starting transfers between devices  93.9 us (49%)
  waiting for transfers between devices  58.1 us (30%)
  Pallas kernels  32.2 us (17%)
  local copies, waits for them, and re-layouts  5.5 us (3%)
    ppermute x27, starting transfers between devices, cyclic(): lax.ppermute(block, 'tensor', [(i, (i + distance) % count) for i in range...  76 us
    ppermute x27, waiting for transfers between devices, cyclic(): lax.ppermute(block, 'tensor', [(i, (i + distance) % count) for i in range...  33.4 us
    pallas_call x12, Pallas kernels, call(): pl.pallas_call(kernel, out_shape=shapes, in_specs=[SMEM_SPEC] + [VMEM_SPE...  25.5 us
    ppermute x8, waiting for transfers between devices, dp_cyclic(): lax.ppermute(block, 'dp', [(i, (i + distance) % count) for i in range(cou...  13.7 us
    ppermute x12, waiting for transfers between devices, gathered_from_below(): result.append(lax.ppermute(block, ('section', 'tensor'), route))  11.1 us
    ppermute x12, starting transfers between devices, gathered_from_below(): result.append(lax.ppermute(block, ('section', 'tensor'), route))  10.2 us
    pallas_call x1, Pallas kernels, update(): pl.pallas_call(functools.partial(update_kernel, pieces, root), grid=(rows...  6.76 us
    ppermute x8, starting transfers between devices, dp_cyclic(): lax.ppermute(block, 'dp', [(i, (i + distance) % count) for i in range(cou...  6.6 us
  transfers between devices with their start and end apart: 50, of which 12 were waited for; matrix products, arithmetic and copies ran while one was open for 1% of the time, Pallas kernels for 13%

profile of v1, /device:TPU:0, one launch (start us, length us, event | category | flops | bytes accessed | tf_op | source)
XLA Modules:
  0.0 192.5 jit_solution(7949837167786243350)
XLA Ops:
  0.6 1.1 slice_bitcast_fusion
  1.8 5.1 %collective-permute-start.17 = (bf16[64,1024]{1,0:T(8,128)(2,1)S(1)}, bf16[64,1024]{1,0:T(8,128)(2,1)S(1)}, u32[]{:S(2)}, u32[]{:S(2)}) collective-permute-start(bf16[64,1024]{1,0:T(8,128)(2,1)S(1)} %get-tuple-element.90.refs_0_.kept_ref), channel_id=1, source_target_pairs={{0,3},{1,0},{2,1},{3,2},{4,7},{5,4},{6,5},{7,6},{8,11},{9,8},{10,9... | collective-permute-start | bytes 393224 | tf_op jit(solution)/shard_map/ppermute | solution.py:23
  7.9 2.8 %collective-permute-start.24 = (bf16[64,1024]{1,0:T(8,128)(2,1)S(1)}, bf16[64,1024]{1,0:T(8,128)(2,1)S(1)}, u32[]{:S(2)}, u32[]{:S(2)}) collective-permute-start(bf16[64,1024]{1,0:T(8,128)(2,1)S(1)} %get-tuple-element.89.refs_0_.kept_ref), channel_id=1, source_target_pairs={{0,3},{1,0},{2,1},{3,2},{4,7},{5,4},{6,5},{7,6},{8,11},{9,8},{10,9... | collective-permute-start | bytes 393224 | tf_op jit(solution)/shard_map/ppermute | solution.py:23
  10.7 1.1 collective-permute-start.23
  11.9 7.8 %collective-permute-done.16.refs_2_ = bf16[64,1024]{1,0:T(8,128)(2,1)S(1)} collective-permute-done((bf16[64,1024]{1,0:T(8,128)(2,1)S(1)}, bf16[64,1024]{1,0:T(8,128)(2,1)S(1)}, u32[]{:S(2)}, u32[]{:S(2)}) %collective-permute-start.16) | collective-permute-done | bytes 131104 | tf_op jit(solution)/shard_map/ppermute | solution.py:23
  19.7 3.4 %copy-done = bf16[1,4096,1024]{2,1,0:T(8,128)(2,1)S(1)} copy-done((bf16[1,4096,1024]{2,1,0:T(8,128)(2,1)S(1)}, bf16[1,4096,1024]{2,1,0:T(8,128)(2,1)}, u32[]{:S(2)}) %copy-start) | copy-done | bytes 8388632
  24.0 3.4 %shard_map.115 = (bf16[64,1152]{1,0:T(8,128)(2,1)S(1)}, bf16[64,1152]{1,0:T(8,128)(2,1)S(1)}, bf16[64,1152]{1,0:T(8,128)(2,1)S(1)}, bf16[64,1152]{1,0:T(8,128)(2...) custom-call(s32[4]{0:T(128)S(1)} %pad_add_fusion.where_ref, ...), custom_call_target="tpu_custom_call" | custom-call | flops 536870912 | bytes 10190864 | tf_op jit(solution)/shard_map/pallas_call | solution.py:190
  27.4 5.6 %collective-permute-start.18 = (bf16[64,1152]{1,0:T(8,128)(2,1)S(1)}, bf16[64,1152]{1,0:T(8,128)(2,1)S(1)}, u32[]{:S(2)}, u32[]{:S(2)}) collective-permute-start(bf16[64,1152]{1,0:T(8,128)(2,1)S(1)} %get-tuple-element.54), channel_id=1, source_target_pairs={{0,1},{1,2},{2,3},{3,0},{4,5},{5,6},{6,7},{7,4},{8,9},{9,10},{10,1... | collective-permute-start | bytes 442376 | tf_op jit(solution)/shard_map/ppermute | solution.py:23
  33.0 2.0 %collective-permute-start.19 = (bf16[64,1152]{1,0:T(8,128)(2,1)S(1)}, bf16[64,1152]{1,0:T(8,128)(2,1)S(1)}, u32[]{:S(2)}, u32[]{:S(2)}) collective-permute-start(bf16[64,1152]{1,0:T(8,128)(2,1)S(1)} %get-tuple-element.55), channel_id=1, source_target_pairs={{0,2},{1,3},{2,0},{3,1},{4,6},{5,7},{6,4},{7,5},{8,10},{9,11},{10,... | collective-permute-start | bytes 442376 | tf_op jit(solution)/shard_map/ppermute | solution.py:23
  35.0 2.8 %collective-permute-start.20 = (bf16[64,1152]{1,0:T(8,128)(2,1)S(1)}, bf16[64,1152]{1,0:T(8,128)(2,1)S(1)}, u32[]{:S(2)}, u32[]{:S(2)}) collective-permute-start(bf16[64,1152]{1,0:T(8,128)(2,1)S(1)} %get-tuple-element.56), channel_id=1, source_target_pairs={{0,3},{1,0},{2,1},{3,2},{4,7},{5,4},{6,5},{7,6},{8,11},{9,8},{10,9... | collective-permute-start | bytes 442376 | tf_op jit(solution)/shard_map/ppermute | solution.py:23
  37.9 7.0 %collective-permute-start.22 = (bf16[64,1024]{1,0:T(8,128)(2,1)S(1)}, bf16[64,1024]{1,0:T(8,128)(2,1)S(1)}, u32[]{:S(2)}, u32[]{:S(2)}) collective-permute-start(bf16[64,1024]{1,0:T(8,128)(2,1)S(1)} %get-tuple-element.89.refs_0_.kept_ref), channel_id=1, source_target_pairs={{0,1},{1,2},{2,3},{3,0},{4,5},{5,6},{6,7},{7,4},{8,9},{9,10},{10,1... | collective-permute-start | bytes 393224 | tf_op jit(solution)/shard_map/ppermute | solution.py:23
  45.8 6.1 %collective-permute-start.2 = (bf16[64,1024]{1,0:T(8,128)(2,1)S(1)}, bf16[64,1024]{1,0:T(8,128)(2,1)S(1)}, u32[]{:S(2)}, u32[]{:S(2)}) collective-permute-start(bf16[64,1024]{1,0:T(8,128)(2,1)S(1)} %bitcast.59), channel_id=1, source_target_pairs={{0,3},{1,0},{2,1},{3,2},{4,7},{5,4},{6,5},{7,6},{8,11},{9,8},{10,9... | collective-permute-start | bytes 393224 | tf_op jit(solution)/shard_map/ppermute | solution.py:23
  52.5 3.4 %shard_map.117 = (bf16[64,1152]{1,0:T(8,128)(2,1)S(1)}, bf16[64,1152]{1,0:T(8,128)(2,1)S(1)}, bf16[64,1152]{1,0:T(8,128)(2,1)S(1)}, bf16[64,1152]{1,0:T(8,128)(2...) custom-call(s32[4]{0:T(128)S(1)} %pad_add_fusion.where_ref, ...), custom_call_target="tpu_custom_call" | custom-call | flops 536870912 | bytes 10190864 | tf_op jit(solution)/shard_map/pallas_call | solution.py:190
  55.9 2.9 %collective-permute-start.25 = (bf16[64,1152]{1,0:T(8,128)(2,1)S(1)}, bf16[64,1152]{1,0:T(8,128)(2,1)S(1)}, u32[]{:S(2)}, u32[]{:S(2)}) collective-permute-start(bf16[64,1152]{1,0:T(8,128)(2,1)S(1)} %get-tuple-element.61), channel_id=1, source_target_pairs={{0,1},{1,2},{2,3},{3,0},{4,5},{5,6},{6,7},{7,4},{8,9},{9,10},{10,1... | collective-permute-start | bytes 442376 | tf_op jit(solution)/shard_map/ppermute | solution.py:23
  59.8 1.5 collective-permute-start.27
  61.4 9.5 %collective-permute-done.1.refs_2_ = bf16[64,1024]{1,0:T(8,128)(2,1)S(1)} collective-permute-done((bf16[64,1024]{1,0:T(8,128)(2,1)S(1)}, bf16[64,1024]{1,0:T(8,128)(2,1)S(1)}, u32[]{:S(2)}, u32[]{:S(2)}) %collective-permute-start.1) | collective-permute-done | bytes 131104 | tf_op jit(solution)/shard_map/ppermute | solution.py:23
  70.8 2.2 %shard_map.111 = (bf16[64,1024]{1,0:T(8,128)(2,1)S(1)}, bf16[64,1024]{1,0:T(8,128)(2,1)S(1)}) custom-call(s32[4]{0:T(128)S(1)} %pad_add_fusion.where_ref, bf16[4096,1024]{1,0:T(8,128)(2,1)S(1)} %bitcast.45, bf16[64,1024]{1,0:T(8,128)(2,1)S(1)} %bitcast.62, bf16[64,1024]{1,0:T(8,128)(2,1)S(1)} %collective-permute-done.refs_1_, ...), custom_call_target="tpu_custom_call" | custom-call | flops 536870912 | bytes 9306128 | tf_op jit(solution)/shard_map/pallas_call | solution.py:190
  73.2 2.6 %collective-permute-start.4 = (bf16[64,1024]{1,0:T(8,128)(2,1)S(1)}, bf16[64,1024]{1,0:T(8,128)(2,1)S(1)}, u32[]{:S(2)}, u32[]{:S(2)}) collective-permute-start(bf16[64,1024]{1,0:T(8,128)(2,1)S(1)} %get-tuple-element.47), channel_id=1, source_target_pairs={{0,9},{1,10},{2,11},{3,8},{8,17},{9,18},{10,19},{11,16},{16,25},{1... | collective-permute-start | bytes 393224 | tf_op jit(solution)/shard_map/ppermute | solution.py:39
  75.8 10.2 %collective-permute-start.31 = (bf16[64,1024]{1,0:T(8,128)(2,1)S(1)}, bf16[64,1024]{1,0:T(8,128)(2,1)S(1)}, u32[]{:S(2)}, u32[]{:S(2)}) collective-permute-start(bf16[64,1024]{1,0:T(8,128)(2,1)S(1)} %get-tuple-element.91.refs_0_.kept_ref), channel_id=1, source_target_pairs={{0,3},{1,0},{2,1},{3,2},{4,7},{5,4},{6,5},{7,6},{8,11},{9,8},{10,9... | collective-permute-start | bytes 393224 | tf_op jit(solution)/shard_map/ppermute | solution.py:23
  86.8 1.5 collective-permute-done.5.refs_2_
  89.4 3.5 %collective-permute-start.38 = (bf16[64,1024]{1,0:T(8,128)(2,1)S(1)}, bf16[64,1024]{1,0:T(8,128)(2,1)S(1)}, u32[]{:S(2)}, u32[]{:S(2)}) collective-permute-start(bf16[64,1024]{1,0:T(8,128)(2,1)S(1)} %get-tuple-element.88.refs_0_.kept_ref), channel_id=1, source_target_pairs={{0,3},{1,0},{2,1},{3,2},{4,7},{5,4},{6,5},{7,6},{8,11},{9,8},{10,9... | collective-permute-start | bytes 393224 | tf_op jit(solution)/shard_map/ppermute | solution.py:23
  92.9 2.2 %shard_map.112 = (bf16[64,1024]{1,0:T(8,128)(2,1)S(1)}, bf16[64,1024]{1,0:T(8,128)(2,1)S(1)}) custom-call(s32[4]{0:T(128)S(1)} %pad_add_fusion.where_ref, bf16[4096,1024]{1,0:T(8,128)(2,1)S(1)} %bitcast.46, bf16[64,1024]{1,0:T(8,128)(2,1)S(1)} %collective-permute-done.3.refs_0_, bf16[64,1024]{1,0:T(8,128)(2,1)S(1)} %collective-permute-done.4.refs_1_, ...), custom_call_target="tpu_custom_call" | custom-call | flops 536870912 | bytes 9306128 | tf_op jit(solution)/shard_map/pallas_call | solution.py:190
  95.2 4.3 %collective-permute-done.30.refs_2_ = bf16[64,1024]{1,0:T(8,128)(2,1)S(1)} collective-permute-done((bf16[64,1024]{1,0:T(8,128)(2,1)S(1)}, bf16[64,1024]{1,0:T(8,128)(2,1)S(1)}, u32[]{:S(2)}, u32[]{:S(2)}) %collective-permute-start.30) | collective-permute-done | bytes 131104 | tf_op jit(solution)/shard_map/ppermute | solution.py:23
  99.5 3.4 %shard_map.119 = (bf16[64,1152]{1,0:T(8,128)(2,1)S(1)}, bf16[64,1152]{1,0:T(8,128)(2,1)S(1)}, bf16[64,1152]{1,0:T(8,128)(2,1)S(1)}, bf16[64,1152]{1,0:T(8,128)(2...) custom-call(s32[4]{0:T(128)S(1)} %pad_add_fusion.where_ref, ...), custom_call_target="tpu_custom_call" | custom-call | flops 536870912 | bytes 10190864 | tf_op jit(solution)/shard_map/pallas_call | solution.py:190
  102.9 5.8 %collective-permute-start.32 = (bf16[64,1152]{1,0:T(8,128)(2,1)S(1)}, bf16[64,1152]{1,0:T(8,128)(2,1)S(1)}, u32[]{:S(2)}, u32[]{:S(2)}) collective-permute-start(bf16[64,1152]{1,0:T(8,128)(2,1)S(1)} %get-tuple-element.68), channel_id=1, source_target_pairs={{0,1},{1,2},{2,3},{3,0},{4,5},{5,6},{6,7},{7,4},{8,9},{9,10},{10,1... | collective-permute-start | bytes 442376 | tf_op jit(solution)/shard_map/ppermute | solution.py:23
  108.7 2.0 %collective-permute-start.33 = (bf16[64,1152]{1,0:T(8,128)(2,1)S(1)}, bf16[64,1152]{1,0:T(8,128)(2,1)S(1)}, u32[]{:S(2)}, u32[]{:S(2)}) collective-permute-start(bf16[64,1152]{1,0:T(8,128)(2,1)S(1)} %get-tuple-element.69), channel_id=1, source_target_pairs={{0,2},{1,3},{2,0},{3,1},{4,6},{5,7},{6,4},{7,5},{8,10},{9,11},{10,... | collective-permute-start | bytes 442376 | tf_op jit(solution)/shard_map/ppermute | solution.py:23
  110.7 2.8 %collective-permute-start.34 = (bf16[64,1152]{1,0:T(8,128)(2,1)S(1)}, bf16[64,1152]{1,0:T(8,128)(2,1)S(1)}, u32[]{:S(2)}, u32[]{:S(2)}) collective-permute-start(bf16[64,1152]{1,0:T(8,128)(2,1)S(1)} %get-tuple-element.70), channel_id=1, source_target_pairs={{0,3},{1,0},{2,1},{3,2},{4,7},{5,4},{6,5},{7,6},{8,11},{9,8},{10,9... | collective-permute-start | bytes 442376 | tf_op jit(solution)/shard_map/ppermute | solution.py:23
  114.6 5.1 %collective-permute-done.33.refs_2_ = bf16[64,1152]{1,0:T(8,128)(2,1)S(1)} collective-permute-done((bf16[64,1152]{1,0:T(8,128)(2,1)S(1)}, bf16[64,1152]{1,0:T(8,128)(2,1)S(1)}, u32[]{:S(2)}, u32[]{:S(2)}) %collective-permute-start.33) | collective-permute-done | bytes 147488 | tf_op jit(solution)/shard_map/ppermute | solution.py:23
  119.7 1.5 collective-permute-start.42
  121.2 6.8 %collective-permute-start.37 = (bf16[64,1024]{1,0:T(8,128)(2,1)S(1)}, bf16[64,1024]{1,0:T(8,128)(2,1)S(1)}, u32[]{:S(2)}, u32[]{:S(2)}) collective-permute-start(bf16[64,1024]{1,0:T(8,128)(2,1)S(1)} %get-tuple-element.88.refs_0_.kept_ref), channel_id=1, source_target_pairs={{0,2},{1,3},{2,0},{3,1},{4,6},{5,7},{6,4},{7,5},{8,10},{9,11},{10,... | collective-permute-start | bytes 393224 | tf_op jit(solution)/shard_map/ppermute | solution.py:23
  129.1 4.3 %collective-permute-start.36 = (bf16[64,1024]{1,0:T(8,128)(2,1)S(1)}, bf16[64,1024]{1,0:T(8,128)(2,1)S(1)}, u32[]{:S(2)}, u32[]{:S(2)}) collective-permute-start(bf16[64,1024]{1,0:T(8,128)(2,1)S(1)} %get-tuple-element.88.refs_0_.kept_ref), channel_id=1, source_target_pairs={{0,1},{1,2},{2,3},{3,0},{4,5},{5,6},{6,7},{7,4},{8,9},{9,10},{10,1... | collective-permute-start | bytes 393224 | tf_op jit(solution)/shard_map/ppermute | solution.py:23
  133.5 1.3 collective-permute-start.46
  134.8 2.2 %shard_map.113 = (bf16[64,1024]{1,0:T(8,128)(2,1)S(1)}, bf16[64,1024]{1,0:T(8,128)(2,1)S(1)}) custom-call(s32[4]{0:T(128)S(1)} %pad_add_fusion.where_ref, bf16[4096,1024]{1,0:T(8,128)(2,1)S(1)} %bitcast.48, bf16[64,1024]{1,0:T(8,128)(2,1)S(1)} %collective-permute-done.7.refs_0_, bf16[64,1024]{1,0:T(8,128)(2,1)S(1)} %collective-permute-done.8.refs_1_, ...), custom_call_target="tpu_custom_call" | custom-call | flops 536870912 | bytes 9306128 | tf_op jit(solution)/shard_map/pallas_call | solution.py:190
  137.0 1.6 collective-permute-done.37.refs_2_
  138.5 1.3 collective-permute-start.14
  139.8 2.1 %collective-permute-start.13 = (bf16[64,1024]{1,0:T(8,128)(2,1)S(1)}, bf16[64,1024]{1,0:T(8,128)(2,1)S(1)}, u32[]{:S(2)}, u32[]{:S(2)}) collective-permute-start(bf16[64,1024]{1,0:T(8,128)(2,1)S(1)} %get-tuple-element.51), channel_id=1, source_target_pairs={{0,10},{1,11},{2,8},{3,9},{8,18},{9,19},{10,16},{11,17},{16,26},{1... | collective-permute-start | bytes 393224 | tf_op jit(solution)/shard_map/ppermute | solution.py:39
  142.0 1.6 collective-permute-start.12
  143.6 3.4 %shard_map.121 = (bf16[64,1152]{1,0:T(8,128)(2,1)S(1)}, bf16[64,1152]{1,0:T(8,128)(2,1)S(1)}, bf16[64,1152]{1,0:T(8,128)(2,1)S(1)}, bf16[64,1152]{1,0:T(8,128)(2...) custom-call(s32[4]{0:T(128)S(1)} %pad_add_fusion.where_ref, ...), custom_call_target="tpu_custom_call" | custom-call | flops 536870912 | bytes 10190864 | tf_op jit(solution)/shard_map/pallas_call | solution.py:190
  147.9 1.3 collective-permute-start.11
  149.3 1.5 collective-permute-start.47
  150.7 9.1 %collective-permute-done.13.refs_2_ = bf16[64,1024]{1,0:T(8,128)(2,1)S(1)} collective-permute-done((bf16[64,1024]{1,0:T(8,128)(2,1)S(1)}, bf16[64,1024]{1,0:T(8,128)(2,1)S(1)}, u32[]{:S(2)}, u32[]{:S(2)}) %collective-permute-start.13) | collective-permute-done | bytes 131104 | tf_op jit(solution)/shard_map/ppermute | solution.py:39
  160.0 2.0 %collective-permute-start.44 = (bf16[2,64,1024]{2,1,0:T(8,128)(2,1)S(1)}, bf16[2,64,1024]{2,1,0:T(8,128)(2,1)S(1)}, u32[]{:S(2)}, u32[]{:S(2)}) collective-permute-start(bf16[2,64,1024]{2,1,0:T(8,128)(2,1)S(1)} %get-tuple-element.83), channel_id=1, source_target_pairs={{0,4},{4,0},{1,5},{5,1},{2,6},{6,2},{3,7},{7,3},{8,12},{12,8},{9,1... | collective-permute-start | bytes 786440 | tf_op jit(solution)/shard_map/ppermute | solution.py:50
  162.2 2.2 %shard_map.114 = bf16[64,1024]{1,0:T(8,128)(2,1)S(1)} custom-call(s32[4]{0:T(128)S(1)} %pad_add_fusion.where_ref, bf16[4096,1024]{1,0:T(8,128)(2,1)S(1)} %bitcast.50, bf16[64,1024]{1,0:T(8,128)(2,1)S(1)} %collective-permute-done.11.refs_0_, bf16[64,1024]{1,0:T(8,128)(2,1)S(1)} %collective-permute-done.12.refs_1_, ...), custom_call_target="tpu_custom_call" | custom-call | flops 536870912 | bytes 9043984 | tf_op jit(solution)/shard_map/pallas_call | solution.py:190
  164.3 3.2 %collective-permute-done.40.refs_2_ = bf16[64,1152]{1,0:T(8,128)(2,1)S(1)} collective-permute-done((bf16[64,1152]{1,0:T(8,128)(2,1)S(1)}, bf16[64,1152]{1,0:T(8,128)(2,1)S(1)}, u32[]{:S(2)}, u32[]{:S(2)}) %collective-permute-start.40) | collective-permute-done | bytes 147488 | tf_op jit(solution)/shard_map/ppermute | solution.py:23
  167.6 1.9 %collective-permute-done.41.refs_3_ = bf16[64,1152]{1,0:T(8,128)(2,1)S(1)} collective-permute-done((bf16[64,1152]{1,0:T(8,128)(2,1)S(1)}, bf16[64,1152]{1,0:T(8,128)(2,1)S(1)}, u32[]{:S(2)}, u32[]{:S(2)}) %collective-permute-start.41) | collective-permute-done | bytes 147488 | tf_op jit(solution)/shard_map/ppermute | solution.py:23
  172.1 11.1 %collective-permute-done.48.refs_13_ = bf16[64,1024]{1,0:T(8,128)(2,1)S(1)} collective-permute-done((bf16[64,1024]{1,0:T(8,128)(2,1)S(1)}, bf16[64,1024]{1,0:T(8,128)(2,1)S(1)}, u32[]{:S(2)}, u32[]{:S(2)}) %collective-permute-start.48) | collective-permute-done | bytes 131104 | tf_op jit(solution)/shard_map/ppermute | solution.py:50
  183.2 2.5 %collective-permute-done.49.refs_15_ = bf16[64,1024]{1,0:T(8,128)(2,1)S(1)} collective-permute-done((bf16[64,1024]{1,0:T(8,128)(2,1)S(1)}, bf16[64,1024]{1,0:T(8,128)(2,1)S(1)}, u32[]{:S(2)}, u32[]{:S(2)}) %collective-permute-start.49) | collective-permute-done | bytes 131104 | tf_op jit(solution)/shard_map/ppermute | solution.py:50
  185.7 6.8 %shard_map.123 = (bf16[2048,1024]{1,0:T(8,128)(2,1)}, bf16[2048,1024]{1,0:T(8,128)(2,1)}) custom-call(bf16[2,64,1024]{2,1,0:T(8,128)(2,1)S(1)} %get-tuple-element.78.refs_0_, bf16[2,64,1024]{2,1,0:T(8,128)(2,1)S(1)} %collective-permute-done.42.refs_1_, bf16[2,64,1024]{2,1,0:T(8,128)(2,1)S(1)} %get-tuple-element.80.refs_2_, ...), custom_call_target="tpu_custom_call" | custom-call | flops 2147483648 | bytes 16777216 | tf_op jit(solution)/shard_map/pallas_call | solution.py:209
  (87 shorter events, 12.6 us)
Async XLA Ops:
  1.8 10.2 %collective-permute-start.17 = (bf16[64,1024]{1,0:T(8,128)(2,1)S(1)}, bf16[64,1024]{1,0:T(8,128)(2,1)S(1)}, u32[]{:S(2)}, u32[]{:S(2)}) collective-permute-start(bf16[64,1024]{1,0:T(8,128)(2,1)S(1)} %get-tuple-element.90.refs_0_.kept_ref), channel_id=1, source_target_pairs={{0,3},{1,0},{2,1},{3,2},{4,7},{5,4},{6,5},{7,6},{8,11},{9,8},{10,9... | collective-permute-start | bytes 393224 | tf_op jit(solution)/shard_map/ppermute | solution.py:23
  6.9 12.8 %collective-permute-start.16 = (bf16[64,1024]{1,0:T(8,128)(2,1)S(1)}, bf16[64,1024]{1,0:T(8,128)(2,1)S(1)}, u32[]{:S(2)}, u32[]{:S(2)}) collective-permute-start(bf16[64,1024]{1,0:T(8,128)(2,1)S(1)} %get-tuple-element.90.refs_0_.kept_ref), channel_id=1, source_target_pairs={{0,2},{1,3},{2,0},{3,1},{4,6},{5,7},{6,4},{7,5},{8,10},{9,11},{10,... | collective-permute-start | bytes 393224 | tf_op jit(solution)/shard_map/ppermute | solution.py:23
  6.9 12.8 %collective-permute-start.15 = (bf16[64,1024]{1,0:T(8,128)(2,1)S(1)}, bf16[64,1024]{1,0:T(8,128)(2,1)S(1)}, u32[]{:S(2)}, u32[]{:S(2)}) collective-permute-start(bf16[64,1024]{1,0:T(8,128)(2,1)S(1)} %get-tuple-element.90.refs_0_.kept_ref), channel_id=1, source_target_pairs={{0,1},{1,2},{2,3},{3,0},{4,5},{5,6},{6,7},{7,4},{8,9},{9,10},{10,1... | collective-permute-start | bytes 393224 | tf_op jit(solution)/shard_map/ppermute | solution.py:23
  7.9 44.0 %collective-permute-start.24 = (bf16[64,1024]{1,0:T(8,128)(2,1)S(1)}, bf16[64,1024]{1,0:T(8,128)(2,1)S(1)}, u32[]{:S(2)}, u32[]{:S(2)}) collective-permute-start(bf16[64,1024]{1,0:T(8,128)(2,1)S(1)} %get-tuple-element.89.refs_0_.kept_ref), channel_id=1, source_target_pairs={{0,3},{1,0},{2,1},{3,2},{4,7},{5,4},{6,5},{7,6},{8,11},{9,8},{10,9... | collective-permute-start | bytes 393224 | tf_op jit(solution)/shard_map/ppermute | solution.py:23
  10.7 41.1 %collective-permute-start.23 = (bf16[64,1024]{1,0:T(8,128)(2,1)S(1)}, bf16[64,1024]{1,0:T(8,128)(2,1)S(1)}, u32[]{:S(2)}, u32[]{:S(2)}) collective-permute-start(bf16[64,1024]{1,0:T(8,128)(2,1)S(1)} %get-tuple-element.89.refs_0_.kept_ref), channel_id=1, source_target_pairs={{0,2},{1,3},{2,0},{3,1},{4,6},{5,7},{6,4},{7,5},{8,10},{9,11},{10,... | collective-permute-start | bytes 393224 | tf_op jit(solution)/shard_map/ppermute | solution.py:23
  27.4 10.5 %collective-permute-start.18 = (bf16[64,1152]{1,0:T(8,128)(2,1)S(1)}, bf16[64,1152]{1,0:T(8,128)(2,1)S(1)}, u32[]{:S(2)}, u32[]{:S(2)}) collective-permute-start(bf16[64,1152]{1,0:T(8,128)(2,1)S(1)} %get-tuple-element.54), channel_id=1, source_target_pairs={{0,1},{1,2},{2,3},{3,0},{4,5},{5,6},{6,7},{7,4},{8,9},{9,10},{10,1... | collective-permute-start | bytes 442376 | tf_op jit(solution)/shard_map/ppermute | solution.py:23
  33.0 11.9 %collective-permute-start.19 = (bf16[64,1152]{1,0:T(8,128)(2,1)S(1)}, bf16[64,1152]{1,0:T(8,128)(2,1)S(1)}, u32[]{:S(2)}, u32[]{:S(2)}) collective-permute-start(bf16[64,1152]{1,0:T(8,128)(2,1)S(1)} %get-tuple-element.55), channel_id=1, source_target_pairs={{0,2},{1,3},{2,0},{3,1},{4,6},{5,7},{6,4},{7,5},{8,10},{9,11},{10,... | collective-permute-start | bytes 442376 | tf_op jit(solution)/shard_map/ppermute | solution.py:23
  35.0 9.9 %collective-permute-start.20 = (bf16[64,1152]{1,0:T(8,128)(2,1)S(1)}, bf16[64,1152]{1,0:T(8,128)(2,1)S(1)}, u32[]{:S(2)}, u32[]{:S(2)}) collective-permute-start(bf16[64,1152]{1,0:T(8,128)(2,1)S(1)} %get-tuple-element.56), channel_id=1, source_target_pairs={{0,3},{1,0},{2,1},{3,2},{4,7},{5,4},{6,5},{7,6},{8,11},{9,8},{10,9... | collective-permute-start | bytes 442376 | tf_op jit(solution)/shard_map/ppermute | solution.py:23
  37.9 14.6 %collective-permute-start.22 = (bf16[64,1024]{1,0:T(8,128)(2,1)S(1)}, bf16[64,1024]{1,0:T(8,128)(2,1)S(1)}, u32[]{:S(2)}, u32[]{:S(2)}) collective-permute-start(bf16[64,1024]{1,0:T(8,128)(2,1)S(1)} %get-tuple-element.89.refs_0_.kept_ref), channel_id=1, source_target_pairs={{0,1},{1,2},{2,3},{3,0},{4,5},{5,6},{6,7},{7,4},{8,9},{9,10},{10,1... | collective-permute-start | bytes 393224 | tf_op jit(solution)/shard_map/ppermute | solution.py:23
  45.8 14.1 %collective-permute-start.2 = (bf16[64,1024]{1,0:T(8,128)(2,1)S(1)}, bf16[64,1024]{1,0:T(8,128)(2,1)S(1)}, u32[]{:S(2)}, u32[]{:S(2)}) collective-permute-start(bf16[64,1024]{1,0:T(8,128)(2,1)S(1)} %bitcast.59), channel_id=1, source_target_pairs={{0,3},{1,0},{2,1},{3,2},{4,7},{5,4},{6,5},{7,6},{8,11},{9,8},{10,9... | collective-permute-start | bytes 393224 | tf_op jit(solution)/shard_map/ppermute | solution.py:23
  51.9 19.0 %collective-permute-start.1 = (bf16[64,1024]{1,0:T(8,128)(2,1)S(1)}, bf16[64,1024]{1,0:T(8,128)(2,1)S(1)}, u32[]{:S(2)}, u32[]{:S(2)}) collective-permute-start(bf16[64,1024]{1,0:T(8,128)(2,1)S(1)} %bitcast.60), channel_id=1, source_target_pairs={{0,2},{1,3},{2,0},{3,1},{4,6},{5,7},{6,4},{7,5},{8,10},{9,11},{10,... | collective-permute-start | bytes 393224 | tf_op jit(solution)/shard_map/ppermute | solution.py:23
  51.9 19.0 %collective-permute-start = (bf16[64,1024]{1,0:T(8,128)(2,1)S(1)}, bf16[64,1024]{1,0:T(8,128)(2,1)S(1)}, u32[]{:S(2)}, u32[]{:S(2)}) collective-permute-start(bf16[64,1024]{1,0:T(8,128)(2,1)S(1)} %bitcast.61), channel_id=1, source_target_pairs={{0,1},{1,2},{2,3},{3,0},{4,5},{5,6},{6,7},{7,4},{8,9},{9,10},{10,1... | collective-permute-start | bytes 393224 | tf_op jit(solution)/shard_map/ppermute | solution.py:23
  55.9 17.2 %collective-permute-start.25 = (bf16[64,1152]{1,0:T(8,128)(2,1)S(1)}, bf16[64,1152]{1,0:T(8,128)(2,1)S(1)}, u32[]{:S(2)}, u32[]{:S(2)}) collective-permute-start(bf16[64,1152]{1,0:T(8,128)(2,1)S(1)} %get-tuple-element.61), channel_id=1, source_target_pairs={{0,1},{1,2},{2,3},{3,0},{4,5},{5,6},{6,7},{7,4},{8,9},{9,10},{10,1... | collective-permute-start | bytes 442376 | tf_op jit(solution)/shard_map/ppermute | solution.py:23
  58.8 16.9 %collective-permute-start.26 = (bf16[64,1152]{1,0:T(8,128)(2,1)S(1)}, bf16[64,1152]{1,0:T(8,128)(2,1)S(1)}, u32[]{:S(2)}, u32[]{:S(2)}) collective-permute-start(bf16[64,1152]{1,0:T(8,128)(2,1)S(1)} %get-tuple-element.62), channel_id=1, source_target_pairs={{0,2},{1,3},{2,0},{3,1},{4,6},{5,7},{6,4},{7,5},{8,10},{9,11},{10,... | collective-permute-start | bytes 442376 | tf_op jit(solution)/shard_map/ppermute | solution.py:23
  59.8 16.0 %collective-permute-start.27 = (bf16[64,1152]{1,0:T(8,128)(2,1)S(1)}, bf16[64,1152]{1,0:T(8,128)(2,1)S(1)}, u32[]{:S(2)}, u32[]{:S(2)}) collective-permute-start(bf16[64,1152]{1,0:T(8,128)(2,1)S(1)} %get-tuple-element.63), channel_id=1, source_target_pairs={{0,3},{1,0},{2,1},{3,2},{4,7},{5,4},{6,5},{7,6},{8,11},{9,8},{10,9... | collective-permute-start | bytes 442376 | tf_op jit(solution)/shard_map/ppermute | solution.py:23
  73.0 13.7 %collective-permute-start.6 = (bf16[64,1024]{1,0:T(8,128)(2,1)S(1)}, bf16[64,1024]{1,0:T(8,128)(2,1)S(1)}, u32[]{:S(2)}, u32[]{:S(2)}) collective-permute-start(bf16[64,1024]{1,0:T(8,128)(2,1)S(1)} %get-tuple-element.47), channel_id=1, source_target_pairs={{0,11},{1,8},{2,9},{3,10},{8,19},{9,16},{10,17},{11,18},{16,27},{1... | collective-permute-start | bytes 393224 | tf_op jit(solution)/shard_map/ppermute | solution.py:39
  73.1 15.3 %collective-permute-start.5 = (bf16[64,1024]{1,0:T(8,128)(2,1)S(1)}, bf16[64,1024]{1,0:T(8,128)(2,1)S(1)}, u32[]{:S(2)}, u32[]{:S(2)}) collective-permute-start(bf16[64,1024]{1,0:T(8,128)(2,1)S(1)} %get-tuple-element.47), channel_id=1, source_target_pairs={{0,10},{1,11},{2,8},{3,9},{8,18},{9,19},{10,16},{11,17},{16,26},{1... | collective-permute-start | bytes 393224 | tf_op jit(solution)/shard_map/ppermute | solution.py:39
  73.2 15.2 %collective-permute-start.4 = (bf16[64,1024]{1,0:T(8,128)(2,1)S(1)}, bf16[64,1024]{1,0:T(8,128)(2,1)S(1)}, u32[]{:S(2)}, u32[]{:S(2)}) collective-permute-start(bf16[64,1024]{1,0:T(8,128)(2,1)S(1)} %get-tuple-element.47), channel_id=1, source_target_pairs={{0,9},{1,10},{2,11},{3,8},{8,17},{9,18},{10,19},{11,16},{16,25},{1... | collective-permute-start | bytes 393224 | tf_op jit(solution)/shard_map/ppermute | solution.py:39
  75.8 13.6 %collective-permute-start.3 = (bf16[64,1024]{1,0:T(8,128)(2,1)S(1)}, bf16[64,1024]{1,0:T(8,128)(2,1)S(1)}, u32[]{:S(2)}, u32[]{:S(2)}) collective-permute-start(bf16[64,1024]{1,0:T(8,128)(2,1)S(1)} %get-tuple-element.47), channel_id=1, source_target_pairs={{0,8},{1,9},{2,10},{3,11},{8,16},{9,17},{10,18},{11,19},{16,24},{1... | collective-permute-start | bytes 393224 | tf_op jit(solution)/shard_map/ppermute | solution.py:39
  75.8 19.3 %collective-permute-start.31 = (bf16[64,1024]{1,0:T(8,128)(2,1)S(1)}, bf16[64,1024]{1,0:T(8,128)(2,1)S(1)}, u32[]{:S(2)}, u32[]{:S(2)}) collective-permute-start(bf16[64,1024]{1,0:T(8,128)(2,1)S(1)} %get-tuple-element.91.refs_0_.kept_ref), channel_id=1, source_target_pairs={{0,3},{1,0},{2,1},{3,2},{4,7},{5,4},{6,5},{7,6},{8,11},{9,8},{10,9... | collective-permute-start | bytes 393224 | tf_op jit(solution)/shard_map/ppermute | solution.py:23
  86.7 12.7 %collective-permute-start.30 = (bf16[64,1024]{1,0:T(8,128)(2,1)S(1)}, bf16[64,1024]{1,0:T(8,128)(2,1)S(1)}, u32[]{:S(2)}, u32[]{:S(2)}) collective-permute-start(bf16[64,1024]{1,0:T(8,128)(2,1)S(1)} %get-tuple-element.91.refs_0_.kept_ref), channel_id=1, source_target_pairs={{0,2},{1,3},{2,0},{3,1},{4,6},{5,7},{6,4},{7,5},{8,10},{9,11},{10,... | collective-permute-start | bytes 393224 | tf_op jit(solution)/shard_map/ppermute | solution.py:23
  88.4 11.1 %collective-permute-start.29 = (bf16[64,1024]{1,0:T(8,128)(2,1)S(1)}, bf16[64,1024]{1,0:T(8,128)(2,1)S(1)}, u32[]{:S(2)}, u32[]{:S(2)}) collective-permute-start(bf16[64,1024]{1,0:T(8,128)(2,1)S(1)} %get-tuple-element.91.refs_0_.kept_ref), channel_id=1, source_target_pairs={{0,1},{1,2},{2,3},{3,0},{4,5},{5,6},{6,7},{7,4},{8,9},{9,10},{10,1... | collective-permute-start | bytes 393224 | tf_op jit(solution)/shard_map/ppermute | solution.py:23
  88.4 11.1 %collective-permute-start.28 = (bf16[64,1024]{1,0:T(8,128)(2,1)S(1)}, bf16[64,1024]{1,0:T(8,128)(2,1)S(1)}, u32[]{:S(2)}, u32[]{:S(2)}) collective-permute-start(bf16[64,1024]{1,0:T(8,128)(2,1)S(1)} %get-tuple-element.65), channel_id=1, source_target_pairs={{0,24},{8,0},{16,8},{24,16},{1,25},{9,1},{17,9},{25,17},{2,26},{10... | collective-permute-start | bytes 393224 | tf_op jit(solution)/shard_map/ppermute | solution.py:45
  89.4 24.1 %collective-permute-start.38 = (bf16[64,1024]{1,0:T(8,128)(2,1)S(1)}, bf16[64,1024]{1,0:T(8,128)(2,1)S(1)}, u32[]{:S(2)}, u32[]{:S(2)}) collective-permute-start(bf16[64,1024]{1,0:T(8,128)(2,1)S(1)} %get-tuple-element.88.refs_0_.kept_ref), channel_id=1, source_target_pairs={{0,3},{1,0},{2,1},{3,2},{4,7},{5,4},{6,5},{7,6},{8,11},{9,8},{10,9... | collective-permute-start | bytes 393224 | tf_op jit(solution)/shard_map/ppermute | solution.py:23
  95.1 18.4 %collective-permute-start.10 = (bf16[64,1024]{1,0:T(8,128)(2,1)S(1)}, bf16[64,1024]{1,0:T(8,128)(2,1)S(1)}, u32[]{:S(2)}, u32[]{:S(2)}) collective-permute-start(bf16[64,1024]{1,0:T(8,128)(2,1)S(1)} %get-tuple-element.49), channel_id=1, source_target_pairs={{0,11},{1,8},{2,9},{3,10},{8,19},{9,16},{10,17},{11,18},{16,27},{1... | collective-permute-start | bytes 393224 | tf_op jit(solution)/shard_map/ppermute | solution.py:39
  102.9 11.7 %collective-permute-start.32 = (bf16[64,1152]{1,0:T(8,128)(2,1)S(1)}, bf16[64,1152]{1,0:T(8,128)(2,1)S(1)}, u32[]{:S(2)}, u32[]{:S(2)}) collective-permute-start(bf16[64,1152]{1,0:T(8,128)(2,1)S(1)} %get-tuple-element.68), channel_id=1, source_target_pairs={{0,1},{1,2},{2,3},{3,0},{4,5},{5,6},{6,7},{7,4},{8,9},{9,10},{10,1... | collective-permute-start | bytes 442376 | tf_op jit(solution)/shard_map/ppermute | solution.py:23
  108.7 11.0 %collective-permute-start.33 = (bf16[64,1152]{1,0:T(8,128)(2,1)S(1)}, bf16[64,1152]{1,0:T(8,128)(2,1)S(1)}, u32[]{:S(2)}, u32[]{:S(2)}) collective-permute-start(bf16[64,1152]{1,0:T(8,128)(2,1)S(1)} %get-tuple-element.69), channel_id=1, source_target_pairs={{0,2},{1,3},{2,0},{3,1},{4,6},{5,7},{6,4},{7,5},{8,10},{9,11},{10,... | collective-permute-start | bytes 442376 | tf_op jit(solution)/shard_map/ppermute | solution.py:23
  110.7 10.5 %collective-permute-start.34 = (bf16[64,1152]{1,0:T(8,128)(2,1)S(1)}, bf16[64,1152]{1,0:T(8,128)(2,1)S(1)}, u32[]{:S(2)}, u32[]{:S(2)}) collective-permute-start(bf16[64,1152]{1,0:T(8,128)(2,1)S(1)} %get-tuple-element.70), channel_id=1, source_target_pairs={{0,3},{1,0},{2,1},{3,2},{4,7},{5,4},{6,5},{7,6},{8,11},{9,8},{10,9... | collective-permute-start | bytes 442376 | tf_op jit(solution)/shard_map/ppermute | solution.py:23
  113.5 15.6 %collective-permute-start.9 = (bf16[64,1024]{1,0:T(8,128)(2,1)S(1)}, bf16[64,1024]{1,0:T(8,128)(2,1)S(1)}, u32[]{:S(2)}, u32[]{:S(2)}) collective-permute-start(bf16[64,1024]{1,0:T(8,128)(2,1)S(1)} %get-tuple-element.49), channel_id=1, source_target_pairs={{0,10},{1,11},{2,8},{3,9},{8,18},{9,19},{10,16},{11,17},{16,26},{1... | collective-permute-start | bytes 393224 | tf_op jit(solution)/shard_map/ppermute | solution.py:39
  113.5 19.9 %collective-permute-start.8 = (bf16[64,1024]{1,0:T(8,128)(2,1)S(1)}, bf16[64,1024]{1,0:T(8,128)(2,1)S(1)}, u32[]{:S(2)}, u32[]{:S(2)}) collective-permute-start(bf16[64,1024]{1,0:T(8,128)(2,1)S(1)} %get-tuple-element.49), channel_id=1, source_target_pairs={{0,9},{1,10},{2,11},{3,8},{8,17},{9,18},{10,19},{11,16},{16,25},{1... | collective-permute-start | bytes 393224 | tf_op jit(solution)/shard_map/ppermute | solution.py:39
  114.6 18.8 %collective-permute-start.7 = (bf16[64,1024]{1,0:T(8,128)(2,1)S(1)}, bf16[64,1024]{1,0:T(8,128)(2,1)S(1)}, u32[]{:S(2)}, u32[]{:S(2)}) collective-permute-start(bf16[64,1024]{1,0:T(8,128)(2,1)S(1)} %get-tuple-element.49), channel_id=1, source_target_pairs={{0,8},{1,9},{2,10},{3,11},{8,16},{9,17},{10,18},{11,19},{16,24},{1... | collective-permute-start | bytes 393224 | tf_op jit(solution)/shard_map/ppermute | solution.py:39
  119.7 28.2 %collective-permute-start.42 = (bf16[2,64,1024]{2,1,0:T(8,128)(2,1)S(1)}, bf16[2,64,1024]{2,1,0:T(8,128)(2,1)S(1)}, u32[]{:S(2)}, u32[]{:S(2)}) collective-permute-start(bf16[2,64,1024]{2,1,0:T(8,128)(2,1)S(1)} %get-tuple-element.79), channel_id=1, source_target_pairs={{0,4},{4,0},{1,5},{5,1},{2,6},{6,2},{3,7},{7,3},{8,12},{12,8},{9,1... | collective-permute-start | bytes 786440 | tf_op jit(solution)/shard_map/ppermute | solution.py:50
  121.2 17.4 %collective-permute-start.37 = (bf16[64,1024]{1,0:T(8,128)(2,1)S(1)}, bf16[64,1024]{1,0:T(8,128)(2,1)S(1)}, u32[]{:S(2)}, u32[]{:S(2)}) collective-permute-start(bf16[64,1024]{1,0:T(8,128)(2,1)S(1)} %get-tuple-element.88.refs_0_.kept_ref), channel_id=1, source_target_pairs={{0,2},{1,3},{2,0},{3,1},{4,6},{5,7},{6,4},{7,5},{8,10},{9,11},{10,... | collective-permute-start | bytes 393224 | tf_op jit(solution)/shard_map/ppermute | solution.py:23
  129.1 10.7 %collective-permute-start.36 = (bf16[64,1024]{1,0:T(8,128)(2,1)S(1)}, bf16[64,1024]{1,0:T(8,128)(2,1)S(1)}, u32[]{:S(2)}, u32[]{:S(2)}) collective-permute-start(bf16[64,1024]{1,0:T(8,128)(2,1)S(1)} %get-tuple-element.88.refs_0_.kept_ref), channel_id=1, source_target_pairs={{0,1},{1,2},{2,3},{3,0},{4,5},{5,6},{6,7},{7,4},{8,9},{9,10},{10,1... | collective-permute-start | bytes 393224 | tf_op jit(solution)/shard_map/ppermute | solution.py:23
  133.4 8.5 %collective-permute-start.35 = (bf16[64,1024]{1,0:T(8,128)(2,1)S(1)}, bf16[64,1024]{1,0:T(8,128)(2,1)S(1)}, u32[]{:S(2)}, u32[]{:S(2)}) collective-permute-start(bf16[64,1024]{1,0:T(8,128)(2,1)S(1)} %get-tuple-element.72), channel_id=1, source_target_pairs={{0,24},{8,0},{16,8},{24,16},{1,25},{9,1},{17,9},{25,17},{2,26},{10... | collective-permute-start | bytes 393224 | tf_op jit(solution)/shard_map/ppermute | solution.py:45
  133.5 13.5 %collective-permute-start.46 = (bf16[64,1024]{1,0:T(8,128)(2,1)S(1)}, bf16[64,1024]{1,0:T(8,128)(2,1)S(1)}, u32[]{:S(2)}, u32[]{:S(2)}) collective-permute-start(bf16[64,1024]{1,0:T(8,128)(2,1)S(1)} %bitcast.55), channel_id=1, source_target_pairs={{0,4},{4,0},{1,5},{5,1},{2,6},{6,2},{3,7},{7,3},{8,12},{12,8},{9,1... | collective-permute-start | bytes 393224 | tf_op jit(solution)/shard_map/ppermute | solution.py:50
  138.5 10.7 %collective-permute-start.14 = (bf16[64,1024]{1,0:T(8,128)(2,1)S(1)}, bf16[64,1024]{1,0:T(8,128)(2,1)S(1)}, u32[]{:S(2)}, u32[]{:S(2)}) collective-permute-start(bf16[64,1024]{1,0:T(8,128)(2,1)S(1)} %get-tuple-element.51), channel_id=1, source_target_pairs={{0,11},{1,8},{2,9},{3,10},{8,19},{9,16},{10,17},{11,18},{16,27},{1... | collective-permute-start | bytes 393224 | tf_op jit(solution)/shard_map/ppermute | solution.py:39
  139.8 20.1 %collective-permute-start.13 = (bf16[64,1024]{1,0:T(8,128)(2,1)S(1)}, bf16[64,1024]{1,0:T(8,128)(2,1)S(1)}, u32[]{:S(2)}, u32[]{:S(2)}) collective-permute-start(bf16[64,1024]{1,0:T(8,128)(2,1)S(1)} %get-tuple-element.51), channel_id=1, source_target_pairs={{0,10},{1,11},{2,8},{3,9},{8,18},{9,19},{10,16},{11,17},{16,26},{1... | collective-permute-start | bytes 393224 | tf_op jit(solution)/shard_map/ppermute | solution.py:39
  142.0 17.9 %collective-permute-start.12 = (bf16[64,1024]{1,0:T(8,128)(2,1)S(1)}, bf16[64,1024]{1,0:T(8,128)(2,1)S(1)}, u32[]{:S(2)}, u32[]{:S(2)}) collective-permute-start(bf16[64,1024]{1,0:T(8,128)(2,1)S(1)} %get-tuple-element.51), channel_id=1, source_target_pairs={{0,9},{1,10},{2,11},{3,8},{8,17},{9,18},{10,19},{11,16},{16,25},{1... | collective-permute-start | bytes 393224 | tf_op jit(solution)/shard_map/ppermute | solution.py:39
  147.0 15.0 %collective-permute-start.39 = (bf16[64,1152]{1,0:T(8,128)(2,1)S(1)}, bf16[64,1152]{1,0:T(8,128)(2,1)S(1)}, u32[]{:S(2)}, u32[]{:S(2)}) collective-permute-start(bf16[64,1152]{1,0:T(8,128)(2,1)S(1)} %get-tuple-element.75), channel_id=1, source_target_pairs={{0,1},{1,2},{2,3},{3,0},{4,5},{5,6},{6,7},{7,4},{8,9},{9,10},{10,1... | collective-permute-start | bytes 442376 | tf_op jit(solution)/shard_map/ppermute | solution.py:23
  147.9 12.0 %collective-permute-start.11 = (bf16[64,1024]{1,0:T(8,128)(2,1)S(1)}, bf16[64,1024]{1,0:T(8,128)(2,1)S(1)}, u32[]{:S(2)}, u32[]{:S(2)}) collective-permute-start(bf16[64,1024]{1,0:T(8,128)(2,1)S(1)} %get-tuple-element.51), channel_id=1, source_target_pairs={{0,8},{1,9},{2,10},{3,11},{8,16},{9,17},{10,18},{11,19},{16,24},{1... | collective-permute-start | bytes 393224 | tf_op jit(solution)/shard_map/ppermute | solution.py:39
  149.3 10.7 %collective-permute-start.47 = (bf16[64,1024]{1,0:T(8,128)(2,1)S(1)}, bf16[64,1024]{1,0:T(8,128)(2,1)S(1)}, u32[]{:S(2)}, u32[]{:S(2)}) collective-permute-start(bf16[64,1024]{1,0:T(8,128)(2,1)S(1)} %collective-permute-done.21.grad_ref.refs_10_), channel_id=1, source_target_pairs={{0,4},{4,0},{1,5},{5,1},{2,6},{6,2},{3,7},{7,3},{8,12},{12,8},{9,1... | collective-permute-start | bytes 393224 | tf_op jit(solution)/shard_map/ppermute | solution.py:50
  159.9 9.6 %collective-permute-start.41 = (bf16[64,1152]{1,0:T(8,128)(2,1)S(1)}, bf16[64,1152]{1,0:T(8,128)(2,1)S(1)}, u32[]{:S(2)}, u32[]{:S(2)}) collective-permute-start(bf16[64,1152]{1,0:T(8,128)(2,1)S(1)} %get-tuple-element.77), channel_id=1, source_target_pairs={{0,3},{1,0},{2,1},{3,2},{4,7},{5,4},{6,5},{7,6},{8,11},{9,8},{10,9... | collective-permute-start | bytes 442376 | tf_op jit(solution)/shard_map/ppermute | solution.py:23
  159.9 12.2 %collective-permute-start.43 = (bf16[2,64,1024]{2,1,0:T(8,128)(2,1)S(1)}, bf16[2,64,1024]{2,1,0:T(8,128)(2,1)S(1)}, u32[]{:S(2)}, u32[]{:S(2)}) collective-permute-start(bf16[2,64,1024]{2,1,0:T(8,128)(2,1)S(1)} %get-tuple-element.81), channel_id=1, source_target_pairs={{0,4},{4,0},{1,5},{5,1},{2,6},{6,2},{3,7},{7,3},{8,12},{12,8},{9,1... | collective-permute-start | bytes 786440 | tf_op jit(solution)/shard_map/ppermute | solution.py:50
  160.0 23.2 %collective-permute-start.44 = (bf16[2,64,1024]{2,1,0:T(8,128)(2,1)S(1)}, bf16[2,64,1024]{2,1,0:T(8,128)(2,1)S(1)}, u32[]{:S(2)}, u32[]{:S(2)}) collective-permute-start(bf16[2,64,1024]{2,1,0:T(8,128)(2,1)S(1)} %get-tuple-element.83), channel_id=1, source_target_pairs={{0,4},{4,0},{1,5},{5,1},{2,6},{6,2},{3,7},{7,3},{8,12},{12,8},{9,1... | collective-permute-start | bytes 786440 | tf_op jit(solution)/shard_map/ppermute | solution.py:50
  162.0 23.7 %collective-permute-start.45 = (bf16[2,64,1024]{2,1,0:T(8,128)(2,1)S(1)}, bf16[2,64,1024]{2,1,0:T(8,128)(2,1)S(1)}, u32[]{:S(2)}, u32[]{:S(2)}) collective-permute-start(bf16[2,64,1024]{2,1,0:T(8,128)(2,1)S(1)} %get-tuple-element.85), channel_id=1, source_target_pairs={{0,4},{4,0},{1,5},{5,1},{2,6},{6,2},{3,7},{7,3},{8,12},{12,8},{9,1... | collective-permute-start | bytes 786440 | tf_op jit(solution)/shard_map/ppermute | solution.py:50
  167.6 15.6 %collective-permute-start.48 = (bf16[64,1024]{1,0:T(8,128)(2,1)S(1)}, bf16[64,1024]{1,0:T(8,128)(2,1)S(1)}, u32[]{:S(2)}, u32[]{:S(2)}) collective-permute-start(bf16[64,1024]{1,0:T(8,128)(2,1)S(1)} %collective-permute-done.28.grad_ref.refs_12_), channel_id=1, source_target_pairs={{0,4},{4,0},{1,5},{5,1},{2,6},{6,2},{3,7},{7,3},{8,12},{12,8},{9,1... | collective-permute-start | bytes 393224 | tf_op jit(solution)/shard_map/ppermute | solution.py:50
  169.5 16.2 %collective-permute-start.49 = (bf16[64,1024]{1,0:T(8,128)(2,1)S(1)}, bf16[64,1024]{1,0:T(8,128)(2,1)S(1)}, u32[]{:S(2)}, u32[]{:S(2)}) collective-permute-start(bf16[64,1024]{1,0:T(8,128)(2,1)S(1)} %collective-permute-done.35.grad_ref.refs_14_), channel_id=1, source_target_pairs={{0,4},{4,0},{1,5},{5,1},{2,6},{6,2},{3,7},{7,3},{8,12},{12,8},{9,1... | collective-permute-start | bytes 393224 | tf_op jit(solution)/shard_map/ppermute | solution.py:50
  (10 other events, 154.2 us)
